TPU v7x, 128 devices: a whole 4x4x4 slice. The times are simulated.
128 devices in a mesh: utt: 8 (over y, core), clu: 16 (over z, x).
Axes of the slice: x: 4, y: 4, z: 4, core: 2. Of those that a mesh axis runs over, the one named last changes fastest.
Arguments:
- features: bfloat16 [262144, 1280], P(('utt', 'clu')), may hold values from -1.75 to 1.75
- centroids: bfloat16 [2048, 1280], P('clu'), may hold values from -2 to 2
- route: int32 [128, 128], P(('utt', 'clu')), may hold values from 0 to 127, each once within a row
Outputs:
- trainer_labels: int32 [128, 128, 16], P(('utt', 'clu'))
- trainer_distance: float32 [128, 128, 16], P(('utt', 'clu'))
Inputs may be any that keep to these rules, and one draw needn't show every extreme that they name: Each row of route names every trainer device exactly once.
All inputs are finite; a program needn't handle non-finite values.
Results may differ from a plain program's by a relative error of at most 0.0003.
Values may be sent and summed in bfloat16 or wider, within the bound.
No kernel may reach another device: no remote copies, remote signals or barrier semaphores. Data moves between devices by JAX's collectives and lax.ppermute only.
A program may use at most 64 MiB of HBM per device.

v0:
```python
import jax
import jax.numpy as jnp
from jax import lax
from jax.sharding import PartitionSpec as P


def per_device(features, centroids, route):
    rows = features.shape[0]
    width = features.shape[1]
    block = 512
    count = rows // block
    feat_blocks = features.reshape(count, block, width)
    frame_sq = jnp.sum(jnp.square(features.astype(jnp.float32)), axis=1).reshape(count, block)
    piece = lax.all_gather(centroids, "clu", axis=0, tiled=True)
    best_dist = jnp.full((count, block), jnp.inf, jnp.float32)
    best_index = jnp.zeros((count, block), jnp.int32)
    cent_sq = jnp.sum(jnp.square(piece.astype(jnp.float32)), axis=1)

    def one_block(items):
        feats, squares, held_dist, held_index = items
        inner = jnp.dot(feats, piece.T, preferred_element_type=jnp.float32)
        dist = (squares[:, None] - 2.0 * inner + cent_sq[None, :]) / width
        found = jnp.min(dist, axis=1)
        where = jnp.argmin(dist, axis=1)
        better = (found < held_dist) | (found == held_dist) & (where < held_index)
        return (jnp.where(better, found, held_dist), jnp.where(better, where, held_index))

    least, labels = lax.map(one_block, (feat_blocks, frame_sq, best_dist, best_index))
    n_utt = lax.axis_size("utt")
    n_clu = lax.axis_size("clu")
    devices = n_utt * n_clu
    per_block = rows // devices
    labels = labels.reshape(devices, per_block)
    least = least.reshape(devices, per_block)
    inverse = jnp.argsort(route[0])
    sent_labels = labels[inverse]
    sent_least = least[inverse]
    got_labels, got_least = (
        lax.all_to_all(sent_labels, ("utt", "clu"), split_axis=0, concat_axis=0, tiled=True),
        lax.all_to_all(sent_least, ("utt", "clu"), split_axis=0, concat_axis=0, tiled=True),
    )
    return (got_labels.reshape(1, devices, per_block), got_least.reshape(1, devices, per_block))


def solution(mesh):
    placed = (P(("utt", "clu"), None), P("clu", None), P(("utt", "clu"), None))
    return jax.shard_map(
        per_device,
        mesh=mesh,
        in_specs=placed,
        out_specs=(P(("utt", "clu"), None, None), P(("utt", "clu"), None, None)),
        check_vma=False,
    )
```

profile of v0, /device:TPU:1, one launch (start us, length us, event | category | flops | bytes accessed | tf_op | source)
XLA Modules:
  0.0 141.9 jit_solution(17112970766078503363)
XLA Ops:
  7.2 0.0 copy-start
  7.2 0.0 all-gather.2.cloned.1.call-start
  7.2 0.7 all-gather.2.cloned.1.call-update
  7.9 3.6 %multiply_reduce_fusion.1 = f32[2048]{0:T(1024)S(1)} fusion(bf16[2048,1280]{1,0:T(8,128)(2,1)} %param.5), kind=kLoop, calls=%fused_computation.11 | loop fusion | flops 7862272 | bytes 5251072 | tf_op jit(solution)/shard_map/reduce_sum | solution.py:13
  11.5 0.0 copy-done
  11.5 2.5 %sort.17 = (s32[128]{0:T(128)}, s32[128]{0:T(128)S(1)}) sort(s32[128]{0:T(128)S(1)} %bitcast.33, s32[128]{0:T(128)S(1)} %iota.11), dimensions={0}, to_apply=%region_5.6 | sort | flops 896 | bytes 2048 | tf_op jit(solution)/shard_map/jit(argsort)/sort | solution.py:35
  14.1 55.5 %all-gather.2.cloned.1.call-done = bf16[2048,1280]{1,0:T(8,128)(2,1)} async-done(((bf16[128,1280]{1,0:T(8,128)(2,1)}), bf16[2048,1280]{1,0:T(8,128)(2,1)}) %all-gather.2.cloned.1.call-update) | async-done | bytes 5242896 | tf_op jit(solution)/shard_map/all_gather | solution.py:14
  69.5 3.6 %multiply_reduce_fusion = f32[2048]{0:T(1024)S(1)} fusion(bf16[2048,1280]{1,0:T(8,128)(2,1)} %all-gather.2.cloned.1.call-done), kind=kLoop, calls=%fused_computation.10 | loop fusion | flops 7862272 | bytes 5251072 | tf_op jit(solution)/shard_map/reduce_sum | solution.py:17
  73.1 28.0 %while.12 = (s32[]{:T(128)}, f32[4,512]{1,0:T(4,128)S(1)}, s32[4,512]{1,0:T(4,128)S(1)}, f32[4,512]{1,0:T(4,128)S(1)}, bf16[4,512,1280]{2,1,0:T(8,128)(2,1)}, /*...) while((s32[]{:T(128)}, f32[4,512]{1,0:T(4,128)S(1)}, s32[4,512]{1,0:T(4,128)S(1)}, ...), condition=%wide.region_4.5_spmd, body=%wide.region_2.4_spmd.sunk | while | flops 2697987584 | bytes 6593129 | solution.py:28
  73.1 6.8 %iota_reduce_fusion.2 = (f32[512]{0:T(512)S(1)}, s32[512]{0:T(512)S(1)}) fusion(bf16[2048,1280]{1,0:T(8,128)(2,1)} %get-tuple-element.137, f32[2048]{0:T(1024)S(1)} %get-tuple-element.138, f32[512]{0:T(512)S(1)} %bitcast.32, bf16[4,512,1280]{2,1,0:T(8,128)(2,1)} %get-tuple-element.136, s32[]{:T(128)} %get-tuple-element.123), kind=kOutput, calls=%fused_computation.2.clone.1 | convolution fusion | flops 2697981440 | bytes 6568448 | tf_op jit(solution)/shard_map/while/body/eval_jaxpr/dot_general | solution.py:21
  80.0 0.1 dynamic_update_slice.11
  80.1 0.1 dynamic_update_slice.10
  80.1 6.8 %iota_reduce_fusion.2 = (f32[512]{0:T(512)S(1)}, s32[512]{0:T(512)S(1)}) fusion(bf16[2048,1280]{1,0:T(8,128)(2,1)} %get-tuple-element.137, f32[2048]{0:T(1024)S(1)} %get-tuple-element.138, f32[512]{0:T(512)S(1)} %bitcast.32, bf16[4,512,1280]{2,1,0:T(8,128)(2,1)} %get-tuple-element.136, s32[]{:T(128)} %get-tuple-element.123), kind=kOutput, calls=%fused_computation.2.clone.1 | convolution fusion | flops 2697981440 | bytes 6568448 | tf_op jit(solution)/shard_map/while/body/eval_jaxpr/dot_general | solution.py:21
  87.0 0.1 dynamic_update_slice.11
  87.0 0.1 dynamic_update_slice.10
  87.1 6.8 %iota_reduce_fusion.2 = (f32[512]{0:T(512)S(1)}, s32[512]{0:T(512)S(1)}) fusion(bf16[2048,1280]{1,0:T(8,128)(2,1)} %get-tuple-element.137, f32[2048]{0:T(1024)S(1)} %get-tuple-element.138, f32[512]{0:T(512)S(1)} %bitcast.32, bf16[4,512,1280]{2,1,0:T(8,128)(2,1)} %get-tuple-element.136, s32[]{:T(128)} %get-tuple-element.123), kind=kOutput, calls=%fused_computation.2.clone.1 | convolution fusion | flops 2697981440 | bytes 6568448 | tf_op jit(solution)/shard_map/while/body/eval_jaxpr/dot_general | solution.py:21
  94.0 0.1 dynamic_update_slice.11
  94.0 0.1 dynamic_update_slice.10
  94.1 6.8 %iota_reduce_fusion.2 = (f32[512]{0:T(512)S(1)}, s32[512]{0:T(512)S(1)}) fusion(bf16[2048,1280]{1,0:T(8,128)(2,1)} %get-tuple-element.137, f32[2048]{0:T(1024)S(1)} %get-tuple-element.138, f32[512]{0:T(512)S(1)} %bitcast.32, bf16[4,512,1280]{2,1,0:T(8,128)(2,1)} %get-tuple-element.136, s32[]{:T(128)} %get-tuple-element.123), kind=kOutput, calls=%fused_computation.2.clone.1 | convolution fusion | flops 2697981440 | bytes 6568448 | tf_op jit(solution)/shard_map/while/body/eval_jaxpr/dot_general | solution.py:21
  101.0 0.1 dynamic_update_slice.11
  101.0 0.1 dynamic_update_slice.10
  101.1 0.1 reshape.33
  101.2 1.2 gather_fusion
  102.4 8.0 %all-to-all-start = ((s32[128,1,16]{2,1,0:T(1,128)}), s32[128,1,16]{2,1,0:T(1,128)S(1)}, u32[]{:S(2)}, u32[]{:S(2)}) async-start(s32[128,1,16]{2,1,0:T(1,128)} %bitcast.7), calls=%async_computation | async-start | bytes 131072 | tf_op jit(solution)/shard_map/all_to_all | solution.py:39
  110.4 0.1 reshape.35
  110.5 1.2 gather_fusion.1
  111.8 8.5 %all-to-all-done = s32[128,1,16]{2,1,0:T(1,128)S(1)} async-done(((s32[128,1,16]{2,1,0:T(1,128)}), s32[128,1,16]{2,1,0:T(1,128)S(1)}, u32[]{:S(2)}, u32[]{:S(2)}) %all-to-all-start) | async-done | bytes 8224 | tf_op jit(solution)/shard_map/all_to_all | solution.py:39
  120.3 4.3 %all-to-all-start.1 = ((f32[128,1,16]{2,1,0:T(1,128)}), f32[128,1,16]{2,1,0:T(1,128)S(1)}, u32[]{:S(2)}, u32[]{:S(2)}) async-start(f32[128,1,16]{2,1,0:T(1,128)} %bitcast.10), calls=%async_computation.1 | async-start | bytes 131072 | tf_op jit(solution)/shard_map/all_to_all | solution.py:40
  124.5 0.7 copy.11
  125.2 9.1 %all-to-all-done.1 = f32[128,1,16]{2,1,0:T(1,128)S(1)} async-done(((f32[128,1,16]{2,1,0:T(1,128)}), f32[128,1,16]{2,1,0:T(1,128)S(1)}, u32[]{:S(2)}, u32[]{:S(2)}) %all-to-all-start.1) | async-done | bytes 8224 | tf_op jit(solution)/shard_map/all_to_all | solution.py:40
  134.4 0.7 copy.12
  (18 shorter events, 0.1 us)
Async XLA Ops:
  7.2 4.4 %copy-start = (s32[1,128]{1,0:T(1,128)S(1)}, s32[1,128]{1,0:T(1,128)}, u32[]{:S(2)}) copy-start(s32[1,128]{1,0:T(1,128)} %param.7) | copy-start | bytes 1540
  7.2 62.4 %all-gather.2.cloned.1.call-start = ((), (), s32[]{:S(2)}) async-start(), calls=%async_computation.2 | async-start | bytes 5570560 | tf_op jit(solution)/shard_map/all_gather | solution.py:14
  102.4 17.8 %all-to-all-start = ((s32[128,1,16]{2,1,0:T(1,128)}), s32[128,1,16]{2,1,0:T(1,128)S(1)}, u32[]{:S(2)}, u32[]{:S(2)}) async-start(s32[128,1,16]{2,1,0:T(1,128)} %bitcast.7), calls=%async_computation | async-start | bytes 131072 | tf_op jit(solution)/shard_map/all_to_all | solution.py:39
  120.3 14.1 %all-to-all-start.1 = ((f32[128,1,16]{2,1,0:T(1,128)}), f32[128,1,16]{2,1,0:T(1,128)S(1)}, u32[]{:S(2)}, u32[]{:S(2)}) async-start(f32[128,1,16]{2,1,0:T(1,128)} %bitcast.10), calls=%async_computation.1 | async-start | bytes 131072 | tf_op jit(solution)/shard_map/all_to_all | solution.py:40
Sparse Core Ops, SparseCore 0:
  10.1 59.3 all-gather.1
where the time goes:
time: 142 us
  waiting for transfers between devices  73.8 us (52%)
  matrix products  27.3 us (19%)
  between operations  14.1 us (10%)
  starting transfers between devices  12.3 us (9%)
  other arithmetic  9.75 us (7%)
  local copies, waits for them, and re-layouts  4.41 us (3%)
    all_gather x1, waiting for transfers between devices, per_device(): piece = lax.all_gather(centroids, 'clu', axis=0, tiled=True)  55.5 us
    dot_general x4, matrix products, one_block(): inner = jnp.dot(feats, piece.T, preferred_element_type=jnp.float32)  27.3 us
    all_to_all x1, waiting for transfers between devices, per_device(): lax.all_to_all(sent_least, ('utt', 'clu'), split_axis=0, concat_axis=0, t...  9.14 us
    all_to_all x1, waiting for transfers between devices, per_device(): lax.all_to_all(sent_labels, ('utt', 'clu'), split_axis=0, concat_axis=0,...  8.49 us
    all_to_all x1, starting transfers between devices, per_device(): lax.all_to_all(sent_labels, ('utt', 'clu'), split_axis=0, concat_axis=0,...  8.03 us
    all_to_all x1, starting transfers between devices, per_device(): lax.all_to_all(sent_least, ('utt', 'clu'), split_axis=0, concat_axis=0, t...  4.28 us
    reduce_sum x1, other arithmetic, per_device(): jnp.sum(jnp.square(features.astype(jnp.float32)), axis=1)  3.58 us
    reduce_sum x1, other arithmetic, per_device(): cent_sq = jnp.sum(jnp.square(piece.astype(jnp.float32)), axis=1)  3.58 us
  transfers between devices with their start and end apart: 3, of which 3 were waited for; matrix products, arithmetic and copies ran while one was open for 6% of the time, Pallas kernels for 0%

commit v1 on v0

--- a/solution.py
+++ b/solution.py
@@ -2,6 +2,27 @@
 import jax.numpy as jnp
 from jax import lax
 from jax.sharding import PartitionSpec as P
+
+
+def gather_around(shard, axis, dim):
+    devices, index, span = (lax.axis_size(axis), lax.axis_index(axis), shard.shape[dim])
+    upward = [(i, (i + 1) % devices) for i in range(devices)]
+    left = [(i, (i - 1) % devices) for i in range(devices)]
+    out = jnp.zeros((*shard.shape[:dim], devices * span, *shard.shape[dim + 1 :]), shard.dtype)
+    out = lax.dynamic_update_slice_in_dim(out, shard, index * span, axis=dim)
+    from_left = from_right = shard
+    halfway = devices // 2
+    for lap in range(1, halfway + 1):
+        from_left = lax.ppermute(from_left, axis, upward)
+        out = lax.dynamic_update_slice_in_dim(
+            out, from_left, (index - lap) % devices * span, axis=dim
+        )
+        if lap < devices - halfway:
+            from_right = lax.ppermute(from_right, axis, left)
+            out = lax.dynamic_update_slice_in_dim(
+                out, from_right, (index + lap) % devices * span, axis=dim
+            )
+    return out
 
 
 def per_device(features, centroids, route):
@@ -11,7 +32,7 @@
     count = rows // block
     feat_blocks = features.reshape(count, block, width)
     frame_sq = jnp.sum(jnp.square(features.astype(jnp.float32)), axis=1).reshape(count, block)
-    piece = lax.all_gather(centroids, "clu", axis=0, tiled=True)
+    piece = gather_around(centroids, "clu", 0)
     best_dist = jnp.full((count, block), jnp.inf, jnp.float32)
     best_index = jnp.zeros((count, block), jnp.int32)
     cent_sq = jnp.sum(jnp.square(piece.astype(jnp.float32)), axis=1)

time: 142 us -> 153 us (1.077)
  starting transfers between devices: 12.3 us -> 52.4 us
  waiting for transfers between devices: 73.8 us -> 58.6 us
  between operations: 14.1 us -> 0.83 us
  other arithmetic: 9.75 us -> 7.31 us
  local copies, waits for them, and re-layouts: 4.41 us -> 6.41 us
    all_gather x1 -> x0, waiting for transfers between devices: 55.5 us -> none  [per_device(): piece = lax.all_gather(centroids, 'clu', axis=0, tiled=True)]
    ppermute x0 -> x15, waiting for transfers between devices: none -> 41 us  [the longest x8 41 us: gather_around(): from_left = lax.ppermute(from_left, axis, upward)]
    ppermute x0 -> x15, starting transfers between devices: none -> 35.6 us  [the longest x7 33.5 us: gather_around(): from_right = lax.ppermute(from_right, axis, left)]
    all_to_all x1, starting transfers between devices: 8.03 us -> 12.5 us  [per_device(): lax.all_to_all(sent_labels, ('utt', 'clu'), split_axis=0, concat_axis=0,...]
    reduce_sum x1, other arithmetic: 3.58 us -> 1.09 us  [per_device(): cent_sq = jnp.sum(jnp.square(piece.astype(jnp.float32)), axis=1)]
  transfers between devices with their start and end apart: 3 -> 17, of which waited for: 3 -> 10; matrix products, arithmetic and copies ran while one was open for 6% -> 6% of each run, Pallas kernels for 0% -> 0%
where the time goes in v1:
time: 153 us
  waiting for transfers between devices  58.6 us (38%)
  starting transfers between devices  52.4 us (34%)
  matrix products  27.3 us (18%)
  other arithmetic  7.31 us (5%)
  local copies, waits for them, and re-layouts  6.41 us (4%)
    ppermute x8, waiting for transfers between devices, gather_around(): from_left = lax.ppermute(from_left, axis, upward)  41 us
    ppermute x7, starting transfers between devices, gather_around(): from_right = lax.ppermute(from_right, axis, left)  33.5 us
    dot_general x4, matrix products, one_block(): inner = jnp.dot(feats, piece.T, preferred_element_type=jnp.float32)  27.3 us
    all_to_all x1, starting transfers between devices, per_device(): lax.all_to_all(sent_labels, ('utt', 'clu'), split_axis=0, concat_axis=0,...  12.5 us
    all_to_all x1, waiting for transfers between devices, per_device(): lax.all_to_all(sent_least, ('utt', 'clu'), split_axis=0, concat_axis=0, t...  9.14 us
    all_to_all x1, waiting for transfers between devices, per_device(): lax.all_to_all(sent_labels, ('utt', 'clu'), split_axis=0, concat_axis=0,...  8.49 us
    all_to_all x1, starting transfers between devices, per_device(): lax.all_to_all(sent_least, ('utt', 'clu'), split_axis=0, concat_axis=0, t...  4.28 us
    reduce_sum x1, other arithmetic, per_device(): jnp.sum(jnp.square(features.astype(jnp.float32)), axis=1)  3.62 us
  transfers between devices with their start and end apart: 17, of which 10 were waited for; matrix products, arithmetic and copies ran while one was open for 6% of the time, Pallas kernels for 0%

profile of v1, /device:TPU:1, one launch (start us, length us, event | category | flops | bytes accessed | tf_op | source)
XLA Modules:
  0.0 153.1 jit_solution(16636548554991904617)
XLA Ops:
  0.6 2.1 %collective-permute-start = (bf16[128,1280]{1,0:T(8,128)(2,1)}, bf16[128,1280]{1,0:T(8,128)(2,1)S(1)}, u32[]{:S(2)}, u32[]{:S(2)}) collective-permute-start(bf16[128,1280]{1,0:T(8,128)(2,1)} %param.6), channel_id=1, source_target_pairs={{0,1},{1,2},{2,3},{3,4},{4,5},{5,6},{6,7},{7,8},{8,9},{9,10},{10,1... | collective-permute-start | bytes 983048 | tf_op jit(solution)/shard_map/ppermute | solution.py:16
  2.7 4.8 %collective-permute-start.1 = (bf16[128,1280]{1,0:T(8,128)(2,1)}, bf16[128,1280]{1,0:T(8,128)(2,1)S(1)}, u32[]{:S(2)}, u32[]{:S(2)}) collective-permute-start(bf16[128,1280]{1,0:T(8,128)(2,1)} %param.6), channel_id=1, source_target_pairs={{0,15},{1,0},{2,1},{3,2},{4,3},{5,4},{6,5},{7,6},{8,7},{9,8},{10,9... | collective-permute-start | bytes 983048 | tf_op jit(solution)/shard_map/ppermute | solution.py:21
  7.6 3.6 %multiply_reduce_fusion.1 = f32[2048]{0:T(1024)S(1)} fusion(bf16[2048,1280]{1,0:T(8,128)(2,1)} %param.5), kind=kLoop, calls=%fused_computation.11 | loop fusion | flops 7862272 | bytes 5251072 | tf_op jit(solution)/shard_map/reduce_sum | solution.py:34
  11.2 2.5 %sort.17 = (s32[128]{0:T(128)}, s32[128]{0:T(128)S(1)}) sort(s32[128]{0:T(128)S(1)} %bitcast.33, s32[128]{0:T(128)S(1)} %iota.11), dimensions={0}, to_apply=%region_5.6 | sort | flops 896 | bytes 2048 | tf_op jit(solution)/shard_map/jit(argsort)/sort | solution.py:56
  13.8 0.3 broadcast_in_dim.22
  14.2 0.9 collective-permute-done
  15.1 4.8 %collective-permute-start.3 = (bf16[128,1280]{1,0:T(8,128)(2,1)S(1)}, bf16[128,1280]{1,0:T(8,128)(2,1)S(1)}, u32[]{:S(2)}, u32[]{:S(2)}) collective-permute-start(bf16[128,1280]{1,0:T(8,128)(2,1)S(1)} %collective-permute-done.1), channel_id=1, source_target_pairs={{0,15},{1,0},{2,1},{3,2},{4,3},{5,4},{6,5},{7,6},{8,7},{9,8},{10,9... | collective-permute-start | bytes 983048 | tf_op jit(solution)/shard_map/ppermute | solution.py:21
  20.0 6.5 %collective-permute-done.2 = bf16[128,1280]{1,0:T(8,128)(2,1)S(1)} collective-permute-done((bf16[128,1280]{1,0:T(8,128)(2,1)S(1)}, bf16[128,1280]{1,0:T(8,128)(2,1)S(1)}, u32[]{:S(2)}, u32[]{:S(2)}) %collective-permute-start.2) | collective-permute-done | bytes 327712 | tf_op jit(solution)/shard_map/ppermute | solution.py:16
  26.4 0.0 collective-permute-start.4
  26.4 0.0 collective-permute-done.3
  26.5 4.8 %collective-permute-start.5 = (bf16[128,1280]{1,0:T(8,128)(2,1)S(1)}, bf16[128,1280]{1,0:T(8,128)(2,1)S(1)}, u32[]{:S(2)}, u32[]{:S(2)}) collective-permute-start(bf16[128,1280]{1,0:T(8,128)(2,1)S(1)} %collective-permute-done.3), channel_id=1, source_target_pairs={{0,15},{1,0},{2,1},{3,2},{4,3},{5,4},{6,5},{7,6},{8,7},{9,8},{10,9... | collective-permute-start | bytes 983048 | tf_op jit(solution)/shard_map/ppermute | solution.py:21
  31.3 5.6 %collective-permute-done.4 = bf16[128,1280]{1,0:T(8,128)(2,1)S(1)} collective-permute-done((bf16[128,1280]{1,0:T(8,128)(2,1)S(1)}, bf16[128,1280]{1,0:T(8,128)(2,1)S(1)}, u32[]{:S(2)}, u32[]{:S(2)}) %collective-permute-start.4) | collective-permute-done | bytes 327712 | tf_op jit(solution)/shard_map/ppermute | solution.py:16
  36.9 4.8 %collective-permute-start.7 = (bf16[128,1280]{1,0:T(8,128)(2,1)S(1)}, bf16[128,1280]{1,0:T(8,128)(2,1)S(1)}, u32[]{:S(2)}, u32[]{:S(2)}) collective-permute-start(bf16[128,1280]{1,0:T(8,128)(2,1)S(1)} %collective-permute-done.5), channel_id=1, source_target_pairs={{0,15},{1,0},{2,1},{3,2},{4,3},{5,4},{6,5},{7,6},{8,7},{9,8},{10,9... | collective-permute-start | bytes 983048 | tf_op jit(solution)/shard_map/ppermute | solution.py:21
  41.8 4.8 %collective-permute-done.6 = bf16[128,1280]{1,0:T(8,128)(2,1)S(1)} collective-permute-done((bf16[128,1280]{1,0:T(8,128)(2,1)S(1)}, bf16[128,1280]{1,0:T(8,128)(2,1)S(1)}, u32[]{:S(2)}, u32[]{:S(2)}) %collective-permute-start.6) | collective-permute-done | bytes 327712 | tf_op jit(solution)/shard_map/ppermute | solution.py:16
  46.6 0.0 collective-permute-start.8
  46.6 4.8 %collective-permute-start.9 = (bf16[128,1280]{1,0:T(8,128)(2,1)S(1)}, bf16[128,1280]{1,0:T(8,128)(2,1)S(1)}, u32[]{:S(2)}, u32[]{:S(2)}) collective-permute-start(bf16[128,1280]{1,0:T(8,128)(2,1)S(1)} %collective-permute-done.7), channel_id=1, source_target_pairs={{0,15},{1,0},{2,1},{3,2},{4,3},{5,4},{6,5},{7,6},{8,7},{9,8},{10,9... | collective-permute-start | bytes 983048 | tf_op jit(solution)/shard_map/ppermute | solution.py:21
  51.4 4.4 %collective-permute-done.8 = bf16[128,1280]{1,0:T(8,128)(2,1)S(1)} collective-permute-done((bf16[128,1280]{1,0:T(8,128)(2,1)S(1)}, bf16[128,1280]{1,0:T(8,128)(2,1)S(1)}, u32[]{:S(2)}, u32[]{:S(2)}) %collective-permute-start.8) | collective-permute-done | bytes 327712 | tf_op jit(solution)/shard_map/ppermute | solution.py:16
  55.8 4.8 %collective-permute-start.11 = (bf16[128,1280]{1,0:T(8,128)(2,1)S(1)}, bf16[128,1280]{1,0:T(8,128)(2,1)S(1)}, u32[]{:S(2)}, u32[]{:S(2)}) collective-permute-start(bf16[128,1280]{1,0:T(8,128)(2,1)S(1)} %collective-permute-done.9), channel_id=1, source_target_pairs={{0,15},{1,0},{2,1},{3,2},{4,3},{5,4},{6,5},{7,6},{8,7},{9,8},{10,9... | collective-permute-start | bytes 983048 | tf_op jit(solution)/shard_map/ppermute | solution.py:21
  60.7 4.4 %collective-permute-done.10 = bf16[128,1280]{1,0:T(8,128)(2,1)S(1)} collective-permute-done((bf16[128,1280]{1,0:T(8,128)(2,1)S(1)}, bf16[128,1280]{1,0:T(8,128)(2,1)S(1)}, u32[]{:S(2)}, u32[]{:S(2)}) %collective-permute-start.10) | collective-permute-done | bytes 327712 | tf_op jit(solution)/shard_map/ppermute | solution.py:16
  65.1 4.8 %collective-permute-start.13 = (bf16[128,1280]{1,0:T(8,128)(2,1)S(1)}, bf16[128,1280]{1,0:T(8,128)(2,1)S(1)}, u32[]{:S(2)}, u32[]{:S(2)}) collective-permute-start(bf16[128,1280]{1,0:T(8,128)(2,1)S(1)} %collective-permute-done.11), channel_id=1, source_target_pairs={{0,15},{1,0},{2,1},{3,2},{4,3},{5,4},{6,5},{7,6},{8,7},{9,8},{10,9... | collective-permute-start | bytes 983048 | tf_op jit(solution)/shard_map/ppermute | solution.py:21
  69.9 4.4 %collective-permute-done.12 = bf16[128,1280]{1,0:T(8,128)(2,1)S(1)} collective-permute-done((bf16[128,1280]{1,0:T(8,128)(2,1)S(1)}, bf16[128,1280]{1,0:T(8,128)(2,1)S(1)}, u32[]{:S(2)}, u32[]{:S(2)}) %collective-permute-start.12) | collective-permute-done | bytes 327712 | tf_op jit(solution)/shard_map/ppermute | solution.py:16
  74.3 0.0 collective-permute-start.14
  74.4 10.0 %collective-permute-done.14 = bf16[128,1280]{1,0:T(8,128)(2,1)S(1)} collective-permute-done((bf16[128,1280]{1,0:T(8,128)(2,1)S(1)}, bf16[128,1280]{1,0:T(8,128)(2,1)S(1)}, u32[]{:S(2)}, u32[]{:S(2)}) %collective-permute-start.14) | collective-permute-done | bytes 327712 | tf_op jit(solution)/shard_map/ppermute | solution.py:16
  84.4 1.1 multiply_reduce_fusion
  85.5 1.2 copy-done
  86.7 28.0 %while.12 = (s32[]{:T(128)}, f32[4,512]{1,0:T(4,128)S(1)}, s32[4,512]{1,0:T(4,128)S(1)}, f32[4,512]{1,0:T(4,128)S(1)}, bf16[4,512,1280]{2,1,0:T(8,128)(2,1)}, /*...) while((s32[]{:T(128)}, f32[4,512]{1,0:T(4,128)S(1)}, s32[4,512]{1,0:T(4,128)S(1)}, ...), condition=%wide.region_4.5_spmd, body=%wide.region_2.4_spmd.sunk | while | flops 2697987584 | bytes 6593129 | solution.py:49
  86.7 6.8 %iota_reduce_fusion.2 = (f32[512]{0:T(512)S(1)}, s32[512]{0:T(512)S(1)}) fusion(bf16[2048,1280]{1,0:T(8,128)(2,1)} %get-tuple-element.137, f32[2048]{0:T(1024)S(1)} %get-tuple-element.138, f32[512]{0:T(512)S(1)} %bitcast.32, bf16[4,512,1280]{2,1,0:T(8,128)(2,1)} %get-tuple-element.136, s32[]{:T(128)} %get-tuple-element.123), kind=kOutput, calls=%fused_computation.2.clone.1 | convolution fusion | flops 2697981440 | bytes 6568448 | tf_op jit(solution)/shard_map/while/body/eval_jaxpr/dot_general | solution.py:42
  93.6 0.1 dynamic_update_slice.91
  93.6 0.1 dynamic_update_slice.90
  93.7 6.8 %iota_reduce_fusion.2 = (f32[512]{0:T(512)S(1)}, s32[512]{0:T(512)S(1)}) fusion(bf16[2048,1280]{1,0:T(8,128)(2,1)} %get-tuple-element.137, f32[2048]{0:T(1024)S(1)} %get-tuple-element.138, f32[512]{0:T(512)S(1)} %bitcast.32, bf16[4,512,1280]{2,1,0:T(8,128)(2,1)} %get-tuple-element.136, s32[]{:T(128)} %get-tuple-element.123), kind=kOutput, calls=%fused_computation.2.clone.1 | convolution fusion | flops 2697981440 | bytes 6568448 | tf_op jit(solution)/shard_map/while/body/eval_jaxpr/dot_general | solution.py:42
  100.6 0.1 dynamic_update_slice.91
  100.6 0.1 dynamic_update_slice.90
  100.7 6.8 %iota_reduce_fusion.2 = (f32[512]{0:T(512)S(1)}, s32[512]{0:T(512)S(1)}) fusion(bf16[2048,1280]{1,0:T(8,128)(2,1)} %get-tuple-element.137, f32[2048]{0:T(1024)S(1)} %get-tuple-element.138, f32[512]{0:T(512)S(1)} %bitcast.32, bf16[4,512,1280]{2,1,0:T(8,128)(2,1)} %get-tuple-element.136, s32[]{:T(128)} %get-tuple-element.123), kind=kOutput, calls=%fused_computation.2.clone.1 | convolution fusion | flops 2697981440 | bytes 6568448 | tf_op jit(solution)/shard_map/while/body/eval_jaxpr/dot_general | solution.py:42
  107.6 0.1 dynamic_update_slice.91
  107.6 0.1 dynamic_update_slice.90
  107.7 6.8 %iota_reduce_fusion.2 = (f32[512]{0:T(512)S(1)}, s32[512]{0:T(512)S(1)}) fusion(bf16[2048,1280]{1,0:T(8,128)(2,1)} %get-tuple-element.137, f32[2048]{0:T(1024)S(1)} %get-tuple-element.138, f32[512]{0:T(512)S(1)} %bitcast.32, bf16[4,512,1280]{2,1,0:T(8,128)(2,1)} %get-tuple-element.136, s32[]{:T(128)} %get-tuple-element.123), kind=kOutput, calls=%fused_computation.2.clone.1 | convolution fusion | flops 2697981440 | bytes 6568448 | tf_op jit(solution)/shard_map/while/body/eval_jaxpr/dot_general | solution.py:42
  114.6 0.1 dynamic_update_slice.91
  114.6 0.1 dynamic_update_slice.90
  114.7 0.1 reshape.33
  114.8 1.2 gather_fusion
  116.0 12.5 %all-to-all-start = ((s32[128,1,16]{2,1,0:T(1,128)}), s32[128,1,16]{2,1,0:T(1,128)S(1)}, u32[]{:S(2)}, u32[]{:S(2)}) async-start(s32[128,1,16]{2,1,0:T(1,128)} %bitcast.7), calls=%async_computation | async-start | bytes 131072 | tf_op jit(solution)/shard_map/all_to_all | solution.py:60
  128.5 0.1 reshape.35
  128.6 1.2 gather_fusion.1
  129.8 8.5 %all-to-all-done = s32[128,1,16]{2,1,0:T(1,128)S(1)} async-done(((s32[128,1,16]{2,1,0:T(1,128)}), s32[128,1,16]{2,1,0:T(1,128)S(1)}, u32[]{:S(2)}, u32[]{:S(2)}) %all-to-all-start) | async-done | bytes 8224 | tf_op jit(solution)/shard_map/all_to_all | solution.py:60
  138.3 4.3 %all-to-all-start.1 = ((f32[128,1,16]{2,1,0:T(1,128)}), f32[128,1,16]{2,1,0:T(1,128)S(1)}, u32[]{:S(2)}, u32[]{:S(2)}) async-start(f32[128,1,16]{2,1,0:T(1,128)} %bitcast.10), calls=%async_computation.1 | async-start | bytes 131072 | tf_op jit(solution)/shard_map/all_to_all | solution.py:61
  142.6 0.7 copy.11
  143.3 9.1 %all-to-all-done.1 = f32[128,1,16]{2,1,0:T(1,128)S(1)} async-done(((f32[128,1,16]{2,1,0:T(1,128)}), f32[128,1,16]{2,1,0:T(1,128)S(1)}, u32[]{:S(2)}, u32[]{:S(2)}) %all-to-all-start.1) | async-done | bytes 8224 | tf_op jit(solution)/shard_map/all_to_all | solution.py:61
  152.4 0.7 copy.12
  (49 shorter events, 0.6 us)
Async XLA Ops:
  0.6 10.6 %copy-start.2 = (s32[1,128]{1,0:T(1,128)S(1)}, s32[1,128]{1,0:T(1,128)}, u32[]{:S(2)}) copy-start(s32[1,128]{1,0:T(1,128)} %param.7) | copy-start | bytes 1540
  0.6 14.5 %collective-permute-start = (bf16[128,1280]{1,0:T(8,128)(2,1)}, bf16[128,1280]{1,0:T(8,128)(2,1)S(1)}, u32[]{:S(2)}, u32[]{:S(2)}) collective-permute-start(bf16[128,1280]{1,0:T(8,128)(2,1)} %param.6), channel_id=1, source_target_pairs={{0,1},{1,2},{2,3},{3,4},{4,5},{5,6},{6,7},{7,8},{8,9},{9,10},{10,1... | collective-permute-start | bytes 983048 | tf_op jit(solution)/shard_map/ppermute | solution.py:16
  2.7 12.4 %collective-permute-start.1 = (bf16[128,1280]{1,0:T(8,128)(2,1)}, bf16[128,1280]{1,0:T(8,128)(2,1)S(1)}, u32[]{:S(2)}, u32[]{:S(2)}) collective-permute-start(bf16[128,1280]{1,0:T(8,128)(2,1)} %param.6), channel_id=1, source_target_pairs={{0,15},{1,0},{2,1},{3,2},{4,3},{5,4},{6,5},{7,6},{8,7},{9,8},{10,9... | collective-permute-start | bytes 983048 | tf_op jit(solution)/shard_map/ppermute | solution.py:21
  7.6 6.6 %copy-start.1 = (bf16[128,1280]{1,0:T(8,128)(2,1)S(1)}, bf16[128,1280]{1,0:T(8,128)(2,1)}, u32[]{:S(2)}) copy-start(bf16[128,1280]{1,0:T(8,128)(2,1)} %param.6) | copy-start | bytes 983044
  15.1 11.3 %collective-permute-start.2 = (bf16[128,1280]{1,0:T(8,128)(2,1)S(1)}, bf16[128,1280]{1,0:T(8,128)(2,1)S(1)}, u32[]{:S(2)}, u32[]{:S(2)}) collective-permute-start(bf16[128,1280]{1,0:T(8,128)(2,1)S(1)} %collective-permute-done), channel_id=1, source_target_pairs={{0,1},{1,2},{2,3},{3,4},{4,5},{5,6},{6,7},{7,8},{8,9},{9,10},{10,1... | collective-permute-start | bytes 983048 | tf_op jit(solution)/shard_map/ppermute | solution.py:16
  15.1 11.3 %collective-permute-start.3 = (bf16[128,1280]{1,0:T(8,128)(2,1)S(1)}, bf16[128,1280]{1,0:T(8,128)(2,1)S(1)}, u32[]{:S(2)}, u32[]{:S(2)}) collective-permute-start(bf16[128,1280]{1,0:T(8,128)(2,1)S(1)} %collective-permute-done.1), channel_id=1, source_target_pairs={{0,15},{1,0},{2,1},{3,2},{4,3},{5,4},{6,5},{7,6},{8,7},{9,8},{10,9... | collective-permute-start | bytes 983048 | tf_op jit(solution)/shard_map/ppermute | solution.py:21
  26.4 10.5 %collective-permute-start.4 = (bf16[128,1280]{1,0:T(8,128)(2,1)S(1)}, bf16[128,1280]{1,0:T(8,128)(2,1)S(1)}, u32[]{:S(2)}, u32[]{:S(2)}) collective-permute-start(bf16[128,1280]{1,0:T(8,128)(2,1)S(1)} %collective-permute-done.2), channel_id=1, source_target_pairs={{0,1},{1,2},{2,3},{3,4},{4,5},{5,6},{6,7},{7,8},{8,9},{9,10},{10,1... | collective-permute-start | bytes 983048 | tf_op jit(solution)/shard_map/ppermute | solution.py:16
  26.5 10.5 %collective-permute-start.5 = (bf16[128,1280]{1,0:T(8,128)(2,1)S(1)}, bf16[128,1280]{1,0:T(8,128)(2,1)S(1)}, u32[]{:S(2)}, u32[]{:S(2)}) collective-permute-start(bf16[128,1280]{1,0:T(8,128)(2,1)S(1)} %collective-permute-done.3), channel_id=1, source_target_pairs={{0,15},{1,0},{2,1},{3,2},{4,3},{5,4},{6,5},{7,6},{8,7},{9,8},{10,9... | collective-permute-start | bytes 983048 | tf_op jit(solution)/shard_map/ppermute | solution.py:21
  36.9 9.6 %collective-permute-start.6 = (bf16[128,1280]{1,0:T(8,128)(2,1)S(1)}, bf16[128,1280]{1,0:T(8,128)(2,1)S(1)}, u32[]{:S(2)}, u32[]{:S(2)}) collective-permute-start(bf16[128,1280]{1,0:T(8,128)(2,1)S(1)} %collective-permute-done.4), channel_id=1, source_target_pairs={{0,1},{1,2},{2,3},{3,4},{4,5},{5,6},{6,7},{7,8},{8,9},{9,10},{10,1... | collective-permute-start | bytes 983048 | tf_op jit(solution)/shard_map/ppermute | solution.py:16
  36.9 9.6 %collective-permute-start.7 = (bf16[128,1280]{1,0:T(8,128)(2,1)S(1)}, bf16[128,1280]{1,0:T(8,128)(2,1)S(1)}, u32[]{:S(2)}, u32[]{:S(2)}) collective-permute-start(bf16[128,1280]{1,0:T(8,128)(2,1)S(1)} %collective-permute-done.5), channel_id=1, source_target_pairs={{0,15},{1,0},{2,1},{3,2},{4,3},{5,4},{6,5},{7,6},{8,7},{9,8},{10,9... | collective-permute-start | bytes 983048 | tf_op jit(solution)/shard_map/ppermute | solution.py:21
  46.6 9.2 %collective-permute-start.8 = (bf16[128,1280]{1,0:T(8,128)(2,1)S(1)}, bf16[128,1280]{1,0:T(8,128)(2,1)S(1)}, u32[]{:S(2)}, u32[]{:S(2)}) collective-permute-start(bf16[128,1280]{1,0:T(8,128)(2,1)S(1)} %collective-permute-done.6), channel_id=1, source_target_pairs={{0,1},{1,2},{2,3},{3,4},{4,5},{5,6},{6,7},{7,8},{8,9},{9,10},{10,1... | collective-permute-start | bytes 983048 | tf_op jit(solution)/shard_map/ppermute | solution.py:16
  46.6 9.2 %collective-permute-start.9 = (bf16[128,1280]{1,0:T(8,128)(2,1)S(1)}, bf16[128,1280]{1,0:T(8,128)(2,1)S(1)}, u32[]{:S(2)}, u32[]{:S(2)}) collective-permute-start(bf16[128,1280]{1,0:T(8,128)(2,1)S(1)} %collective-permute-done.7), channel_id=1, source_target_pairs={{0,15},{1,0},{2,1},{3,2},{4,3},{5,4},{6,5},{7,6},{8,7},{9,8},{10,9... | collective-permute-start | bytes 983048 | tf_op jit(solution)/shard_map/ppermute | solution.py:21
  55.8 9.2 %collective-permute-start.10 = (bf16[128,1280]{1,0:T(8,128)(2,1)S(1)}, bf16[128,1280]{1,0:T(8,128)(2,1)S(1)}, u32[]{:S(2)}, u32[]{:S(2)}) collective-permute-start(bf16[128,1280]{1,0:T(8,128)(2,1)S(1)} %collective-permute-done.8), channel_id=1, source_target_pairs={{0,1},{1,2},{2,3},{3,4},{4,5},{5,6},{6,7},{7,8},{8,9},{9,10},{10,1... | collective-permute-start | bytes 983048 | tf_op jit(solution)/shard_map/ppermute | solution.py:16
  55.8 9.2 %collective-permute-start.11 = (bf16[128,1280]{1,0:T(8,128)(2,1)S(1)}, bf16[128,1280]{1,0:T(8,128)(2,1)S(1)}, u32[]{:S(2)}, u32[]{:S(2)}) collective-permute-start(bf16[128,1280]{1,0:T(8,128)(2,1)S(1)} %collective-permute-done.9), channel_id=1, source_target_pairs={{0,15},{1,0},{2,1},{3,2},{4,3},{5,4},{6,5},{7,6},{8,7},{9,8},{10,9... | collective-permute-start | bytes 983048 | tf_op jit(solution)/shard_map/ppermute | solution.py:21
  65.0 9.2 %collective-permute-start.12 = (bf16[128,1280]{1,0:T(8,128)(2,1)S(1)}, bf16[128,1280]{1,0:T(8,128)(2,1)S(1)}, u32[]{:S(2)}, u32[]{:S(2)}) collective-permute-start(bf16[128,1280]{1,0:T(8,128)(2,1)S(1)} %collective-permute-done.10), channel_id=1, source_target_pairs={{0,1},{1,2},{2,3},{3,4},{4,5},{5,6},{6,7},{7,8},{8,9},{9,10},{10,1... | collective-permute-start | bytes 983048 | tf_op jit(solution)/shard_map/ppermute | solution.py:16
  65.1 9.3 %collective-permute-start.13 = (bf16[128,1280]{1,0:T(8,128)(2,1)S(1)}, bf16[128,1280]{1,0:T(8,128)(2,1)S(1)}, u32[]{:S(2)}, u32[]{:S(2)}) collective-permute-start(bf16[128,1280]{1,0:T(8,128)(2,1)S(1)} %collective-permute-done.11), channel_id=1, source_target_pairs={{0,15},{1,0},{2,1},{3,2},{4,3},{5,4},{6,5},{7,6},{8,7},{9,8},{10,9... | collective-permute-start | bytes 983048 | tf_op jit(solution)/shard_map/ppermute | solution.py:21
  74.3 10.1 %collective-permute-start.14 = (bf16[128,1280]{1,0:T(8,128)(2,1)S(1)}, bf16[128,1280]{1,0:T(8,128)(2,1)S(1)}, u32[]{:S(2)}, u32[]{:S(2)}) collective-permute-start(bf16[128,1280]{1,0:T(8,128)(2,1)S(1)} %collective-permute-done.12), channel_id=1, source_target_pairs={{0,1},{1,2},{2,3},{3,4},{4,5},{5,6},{6,7},{7,8},{8,9},{9,10},{10,1... | collective-permute-start | bytes 983048 | tf_op jit(solution)/shard_map/ppermute | solution.py:16
  84.4 2.3 %copy-start = (bf16[2048,1280]{1,0:T(8,128)(2,1)}, bf16[2048,1280]{1,0:T(8,128)(2,1)S(1)}, u32[]{:S(2)}) copy-start(bf16[2048,1280]{1,0:T(8,128)(2,1)S(1)} %constant_dynamic-update-slice_fusion) | copy-start | bytes 15728644
  116.0 22.3 %all-to-all-start = ((s32[128,1,16]{2,1,0:T(1,128)}), s32[128,1,16]{2,1,0:T(1,128)S(1)}, u32[]{:S(2)}, u32[]{:S(2)}) async-start(s32[128,1,16]{2,1,0:T(1,128)} %bitcast.7), calls=%async_computation | async-start | bytes 131072 | tf_op jit(solution)/shard_map/all_to_all | solution.py:60
  138.3 14.1 %all-to-all-start.1 = ((f32[128,1,16]{2,1,0:T(1,128)}), f32[128,1,16]{2,1,0:T(1,128)S(1)}, u32[]{:S(2)}, u32[]{:S(2)}) async-start(f32[128,1,16]{2,1,0:T(1,128)} %bitcast.10), calls=%async_computation.1 | async-start | bytes 131072 | tf_op jit(solution)/shard_map/all_to_all | solution.py:61
